TPU v7x, 32 devices: a whole 2x2x4 slice. The times are simulated.
32 devices in a mesh: band: 8 (over y, x, core), chan: 4 (over z).
Axes of the slice: x: 2, y: 2, z: 4, core: 2. Of those that a mesh axis runs over, the one named last changes fastest.
Arguments:
- grid_feat: bfloat16 [2048, 468], P('band'), may hold values from -6 to 6
- w_embed: bfloat16 [468, 384], replicated, may hold values from -0.25 to 0.25
- w_send: bfloat16 [384, 384], P(None, 'chan'), may hold values from -0.3125 to 0.3125
- w_recv: bfloat16 [384, 384], P(None, 'chan'), may hold values from -0.3125 to 0.3125
- mesh_nodes: bfloat16 [2048, 384], P('band'), may hold values from -6 to 6
- mesh_cot: bfloat16 [2048, 384], P('band', 'chan'), may hold values from -0.049804688 to 0.049804688
- send_index: int32 [8, 2, 64], P('band'), may hold values from -1 to 255, as said below
- edge_source: int32 [32768], P('band'), may hold values from 0 to 383, as said below
- edge_receiver: int32 [32768], P('band'), may hold values from 0 to 255
Outputs:
- mesh_out: bfloat16 [2048, 384], P('band', 'chan')
- grad_embed: float32 [468, 384], P(None, 'chan')
- grad_send: float32 [384, 384], P(None, 'chan')
- grad_recv: float32 [384, 384], P(None, 'chan')
Inputs may be any that keep to these rules, and one draw needn't show every extreme that they name: `send_index`: A block's first c slots hold rows (c from 32 to 64) and the rest hold -1; block [0, 0] and block [8 - 1, 1] hold only -1; for every band s one of its two blocks that are not all -1 has all 64 slots used (block [0, 1] for band 0, block [8 - 1, 0] for band 8 - 1). `edge_source`: every edge names a used slot of its partition, and every used slot is named by some edge of its partition.
All inputs are finite; a program needn't handle non-finite values.
Results may differ from a plain program's by a relative error of at most 0.011.
Values may be sent and summed in bfloat16 or wider, within the bound.
A program may use at most 64 MiB of HBM per device.

v0:
```python
import jax
import jax.numpy as jnp
from jax import lax
from jax.sharding import PartitionSpec as P


def extended(cells, sides, width):
    for axis, dim in sides:
        count = lax.axis_size(axis)
        ends = count - 1
        head = lax.slice_in_dim(cells, 0, width, axis=dim)
        tail = lax.slice_in_dim(cells, cells.shape[dim] - width, cells.shape[dim], axis=dim)
        cells = jnp.concatenate(
            [
                lax.ppermute(tail, axis, [(i, (i + 1) % count) for i in range(ends)]),
                cells,
                lax.ppermute(head, axis, [((i + 1) % count, i) for i in range(ends)]),
            ],
            axis=dim,
        )
    return cells


def silu_slope(inputs):
    sigmoid_v = jax.nn.sigmoid(inputs)
    return sigmoid_v * (1.0 + inputs * (1.0 - sigmoid_v))


def on_device(
    grid_feat, w_embed, w_send, w_recv, mesh_nodes, mesh_cot, send_index, edge_source, edge_receiver
):
    chan_count = lax.axis_size("chan")
    chan_index = lax.axis_index("chan")
    latent_width = w_embed.shape[1]
    part_width = latent_width // chan_count
    grid_count = grid_feat.shape[0]
    mesh_count = mesh_nodes.shape[0]
    send_rows = send_index[0]
    block_slots = send_rows.shape[1]
    slot_total = grid_count + 2 * block_slots
    occupied = send_rows >= 0
    safe_rows = jnp.maximum(send_rows, 0)
    grid_pre = jnp.dot(grid_feat, w_embed, preferred_element_type=jnp.float32)
    latent = jax.nn.silu(grid_pre).astype(jnp.bfloat16)
    outgoing = jnp.where(occupied[:, :, None], latent[safe_rows], jnp.zeros((), jnp.bfloat16))
    bordered = extended(outgoing, (("band", 0),), 1)
    received = jnp.concatenate([latent, bordered[0], bordered[3]], axis=0)
    pre_mine = lax.dynamic_slice_in_dim(grid_pre, chan_index * part_width, part_width, 1)
    send_proj = jnp.dot(received, w_send, preferred_element_type=jnp.float32)
    recv_proj = jnp.dot(mesh_nodes, w_recv, preferred_element_type=jnp.float32)
    edge_pre = send_proj[edge_source] + recv_proj[edge_receiver]
    message = jax.nn.silu(edge_pre).astype(jnp.bfloat16)
    mesh_out = jax.ops.segment_sum(message.astype(jnp.float32), edge_receiver, mesh_count).astype(
        jnp.bfloat16
    )
    edge_grad = (mesh_cot[edge_receiver].astype(jnp.float32) * silu_slope(edge_pre)).astype(
        jnp.bfloat16
    )
    slot_grad = jax.ops.segment_sum(edge_grad.astype(jnp.float32), edge_source, slot_total).astype(
        jnp.bfloat16
    )
    recv_grad = jax.ops.segment_sum(
        edge_grad.astype(jnp.float32), edge_receiver, mesh_count
    ).astype(jnp.bfloat16)
    send_part = jnp.einsum("rk,rh->kh", received, slot_grad, preferred_element_type=jnp.float32)
    recv_part = jnp.einsum("mk,mh->kh", mesh_nodes, recv_grad, preferred_element_type=jnp.float32)
    partial_back = jnp.einsum("rh,kh->rk", slot_grad, w_send, preferred_element_type=jnp.float32)
    slot_back = lax.psum_scatter(partial_back, "chan", scatter_dimension=1, tiled=True)
    own_back = slot_back[:grid_count]
    outward = slot_back[grid_count:].reshape(2, block_slots, part_width)
    bordered_back = extended(outward, (("band", 0),), 1)
    returned = jnp.concatenate([bordered_back[0], bordered_back[3]], axis=0)
    row_ids = jnp.where(occupied, send_rows, grid_count).reshape(-1)
    grid_grad = own_back + jax.ops.segment_sum(returned, row_ids, grid_count)
    pre_grad = (grid_grad * silu_slope(pre_mine)).astype(jnp.bfloat16)
    embed_part = jnp.einsum("gf,gl->fl", grid_feat, pre_grad, preferred_element_type=jnp.float32)
    grad_embed, grad_send, grad_recv = lax.psum((embed_part, send_part, recv_part), "band")
    return (mesh_out, grad_embed, grad_send, grad_recv)


def solution(mesh):
    placed = (
        P("band", None),
        P(),
        P(None, "chan"),
        P(None, "chan"),
        P("band", None),
        P("band", "chan"),
        P("band", None, None),
        P("band"),
        P("band"),
    )
    return jax.shard_map(
        on_device,
        mesh=mesh,
        in_specs=placed,
        out_specs=(P("band", "chan"), P(None, "chan"), P(None, "chan"), P(None, "chan")),
        check_vma=False,
    )
```

profile of v0, /device:TPU:0, one launch (start us, length us, event | category | flops | bytes accessed | tf_op | source)
XLA Modules:
  0.0 192.6 jit_solution(4992135359315319195)
XLA Ops:
  7.3 0.8 compare_bitcast_fusion
  8.8 2.0 %multiply_convert_fusion.3 = (bf16[256,384]{1,0:T(8,128)(2,1)S(1)}, f32[256,384]{1,0:T(8,128)}) fusion(bf16[256,468]{0,1:T(8,128)(2,1)} %param.9, bf16[468,384]{1,0:T(8,128)(2,1)S(1)} %copy-done), kind=kOutput, calls=%fused_computation.21 | convolution fusion | flops 92504064 | bytes 1188864 | tf_op jit(solution)/shard_map/dot_general | solution.py:43
  10.8 0.9 gather_fusion
  11.8 2.4 %collective-permute-start = (bf16[1,64,384]{2,1,0:T(8,128)(2,1)S(1)}, bf16[1,64,384]{2,1,0:T(8,128)(2,1)S(1)}, u32[]{:S(2)}, u32[]{:S(2)}) collective-permute-start(bf16[1,64,384]{2,1,0:T(8,128)(2,1)S(1)} %get-tuple-element.17), channel_id=1, source_target_pairs={{0,4},{4,8},{8,12},{12,16},{16,20},{20,24},{24,28},{1,5},{5,9},{9,... | collective-permute-start | bytes 147464 | tf_op jit(solution)/shard_map/ppermute | solution.py:15
  14.2 1.3 collective-permute-start.1
  15.9 15.0 %gather_fusion.3 = bf16[4096,96]{1,0:T(8,128)(2,1)} fusion(bf16[256,96]{1,0:T(8,128)(2,1)S(1)} %copy.24, s32[4096]{0:T(1024)S(1)} %fusion.21), kind=kCustom, calls=%fused_computation.3 | custom fusion | bytes 1589248 | tf_op jit(solution)/shard_map/gather | solution.py:56
  31.0 10.8 %gather_fusion.2 = f32[4096,96]{1,0:T(8,128)S(1)} fusion(f32[256,96]{1,0:T(8,128)S(1)} %fusion.29, s32[4096]{0:T(1024)S(1)} %fusion.21), kind=kCustom, calls=%fused_computation.2 | custom fusion | bytes 3162112 | tf_op jit(solution)/shard_map/gather | solution.py:51
  42.4 14.2 %gather_fusion.1 = f32[4096,96]{1,0:T(8,128)} fusion(f32[384,96]{1,0:T(8,128)S(1)} %fusion.8, s32[4096]{0:T(1024)S(1)} %fusion.20), kind=kCustom, calls=%fused_computation.1 | custom fusion | bytes 3162112 | tf_op jit(solution)/shard_map/gather | solution.py:51
  56.6 24.4 %scatter_custom_fusion.1 = f32[384,96]{1,0:T(8,128)} fusion(s32[4096]{0:T(1024)S(1)} %copy-done.7, f32[]{:T(128)} %constant.8.clone.1, bf16[4096,96]{1,0:T(8,128)(2,1)} %gather_fusion.3, f32[4096,96]{1,0:T(8,128)} %gather_fusion.1, f32[4096,96]{1,0:T(8,128)S(1)} %gather_fusion.2), kind=kCustom, calls=%fused_computation.10 | custom fusion | flops 5111808 | bytes 4603908 | tf_op jit(solution)/shard_map/scatter-add | solution.py:59
  80.9 2.1 %convolution_bitcast_fusion = f32[384,384]{1,0:T(8,128)} fusion(bf16[384,96]{0,1:T(8,128)(2,1)} %param.11, f32[384,96]{1,0:T(8,128)} %scatter_custom_fusion.1), kind=kOutput, calls=%fused_computation.17 | convolution fusion | flops 28348416 | bytes 811008
  83.2 24.2 %scatter_custom_fusion.3 = f32[256,96]{1,0:T(8,128)} fusion(s32[4096]{0:T(1024)S(1)} %copy-done.8, f32[]{:T(128)} %constant.8.clone.1, bf16[4096,96]{1,0:T(8,128)(2,1)S(1)} %copy-done.1, f32[4096,96]{1,0:T(8,128)} %gather_fusion.1, f32[4096,96]{1,0:T(8,128)S(1)} %gather_fusion.2), kind=kCustom, calls=%fused_computation.8 | custom fusion | flops 5111808 | bytes 4816900 | tf_op jit(solution)/shard_map/scatter-add | solution.py:62
  107.4 1.9 convolution_bitcast_fusion.2
  110.0 0.9 fusion.27
  111.1 1.3 collective-permute-start.3
  112.4 5.1 %collective-permute-start.2 = (f32[1,64,96]{2,1,0:T(8,128)S(1)}, f32[1,64,96]{2,1,0:T(8,128)S(1)}, u32[]{:S(2)}, u32[]{:S(2)}) collective-permute-start(f32[1,64,96]{2,1,0:T(8,128)S(1)} %bitcast.29), channel_id=1, source_target_pairs={{0,4},{4,8},{8,12},{12,16},{16,20},{20,24},{24,28},{1,5},{5,9},{9,... | collective-permute-start | bytes 73736 | tf_op jit(solution)/shard_map/ppermute | solution.py:15
  117.5 2.0 %fusion.7 = f32[384,96]{0,1:T(8,128)} fusion(bf16[64,384]{1,0:T(8,128)(2,1)} %bitcast.36, bf16[64,384]{1,0:T(8,128)(2,1)} %bitcast.34, bf16[256,384]{1,0:T(8,128)(2,1)} %copy-done.2, f32[384,96]{1,0:T(8,128)} %scatter_custom_fusion.1), kind=kOutput, calls=%fused_computation.24 | convolution fusion | flops 29233152 | bytes 589824 | tf_op jit(solution)/shard_map/rk,rh->kh/dot_general | solution.py:65
  119.5 0.9 slice.41
  120.5 1.3 scatter_custom_fusion.2
  121.8 2.0 %convolution_bitcast_fusion.1 = f32[468,96]{0,1:T(8,128)} fusion(bf16[256,468]{0,1:T(8,128)(2,1)S(1)} %copy-done.10, f32[256,96]{1,0:T(8,128)S(1)} %scatter_custom_fusion.2, f32[256,384]{1,0:T(8,128)} %get-tuple-element.20, s32[]{:T(128)S(6)} %select_n.30), kind=kOutput, calls=%fused_computation.18 | convolution fusion | flops 23224320 | bytes 648708 | tf_op jit(solution)/shard_map/gf,gl->fl/dot_general | solution.py:76
  123.8 23.4 %scatter_custom_fusion = f32[256,96]{1,0:T(8,128)S(1)} fusion(s32[4096]{0:T(1024)S(1)} %copy-done.8, f32[]{:T(128)} %constant.9.clone.1, f32[4096,96]{1,0:T(8,128)} %gather_fusion.1, f32[4096,96]{1,0:T(8,128)S(1)} %gather_fusion.2, f32[]{:T(128)} %constant.8.clone.1), kind=kCustom, calls=%fused_computation.13 | custom fusion | flops 3145728 | bytes 3768328 | tf_op jit(solution)/shard_map/scatter-add | solution.py:53
  147.9 33.0 %all-reduce.3.cloned.1.call-done = (f32[468,96]{0,1:T(8,128)}, f32[384,96]{0,1:T(8,128)}, f32[384,96]{0,1:T(8,128)}) async-done(((f32[468,96]{0,1:T(8,128)}, f32[384,96]{0,1:T(8,128)}, f32[384,96]{0,1:T(8,128)}), (f32[468,96]{0,1:T(8,128)}, f32[384,96]{0,1:T(8,128)}, f32[384,96]{0,1:T(8,128)})) %all-reduce.3.cloned.1.call-update) | async-done | bytes 474640 | tf_op jit(solution)/shard_map/psum | solution.py:77
  181.0 1.6 copy.39
  182.6 1.6 copy.40
  184.1 1.6 copy.41
  (52 shorter events, 3.7 us)
Async XLA Ops:
  7.2 1.6 copy-start
  7.2 8.3 %copy-start.8 = (s32[4096]{0:T(1024)S(1)}, s32[4096]{0:T(1024)}, u32[]{:S(2)}) copy-start(s32[4096]{0:T(1024)} %param.17) | copy-start | bytes 49156
  7.2 8.4 %copy-start.3 = (bf16[256,384]{1,0:T(8,128)(2,1)S(1)}, bf16[256,384]{1,0:T(8,128)(2,1)}, u32[]{:S(2)}) copy-start(bf16[256,384]{1,0:T(8,128)(2,1)} %param.13) | copy-start | bytes 589828
  7.2 8.4 %copy-start.4 = (bf16[384,96]{0,1:T(8,128)(2,1)S(1)}, bf16[384,96]{0,1:T(8,128)(2,1)}, u32[]{:S(2)}) copy-start(bf16[384,96]{0,1:T(8,128)(2,1)} %param.12) | copy-start | bytes 221188
  7.2 102.8 %reduce-scatter.4.cloned.1.call-start = ((), (), s32[]{:S(2)}) async-start(), calls=%async_computation.1 | async-start | bytes 737280
  8.8 7.0 %copy-start.7 = (s32[4096]{0:T(1024)S(1)}, s32[4096]{0:T(1024)}, u32[]{:S(2)}) copy-start(s32[4096]{0:T(1024)} %param.16) | copy-start | bytes 49156
  8.8 7.0 %copy-start.6 = (bf16[256,96]{0,1:T(8,128)(2,1)S(1)}, bf16[256,96]{0,1:T(8,128)(2,1)}, u32[]{:S(2)}) copy-start(bf16[256,96]{0,1:T(8,128)(2,1)} %param.14) | copy-start | bytes 147460
  10.8 31.0 %copy-start.2 = (bf16[256,384]{1,0:T(8,128)(2,1)}, bf16[256,384]{1,0:T(8,128)(2,1)S(1)}, u32[]{:S(2)}) copy-start(bf16[256,384]{1,0:T(8,128)(2,1)S(1)} %get-tuple-element.19) | copy-start | bytes 589828
  11.8 29.9 %collective-permute-start = (bf16[1,64,384]{2,1,0:T(8,128)(2,1)S(1)}, bf16[1,64,384]{2,1,0:T(8,128)(2,1)S(1)}, u32[]{:S(2)}, u32[]{:S(2)}) collective-permute-start(bf16[1,64,384]{2,1,0:T(8,128)(2,1)S(1)} %get-tuple-element.17), channel_id=1, source_target_pairs={{0,4},{4,8},{8,12},{12,16},{16,20},{20,24},{24,28},{1,5},{5,9},{9,... | collective-permute-start | bytes 147464 | tf_op jit(solution)/shard_map/ppermute | solution.py:15
  14.2 27.5 %collective-permute-start.1 = (bf16[1,64,384]{2,1,0:T(8,128)(2,1)S(1)}, bf16[1,64,384]{2,1,0:T(8,128)(2,1)S(1)}, u32[]{:S(2)}, u32[]{:S(2)}) collective-permute-start(bf16[1,64,384]{2,1,0:T(8,128)(2,1)S(1)} %get-tuple-element.18), channel_id=1, source_target_pairs={{4,0},{8,4},{12,8},{16,12},{20,16},{24,20},{28,24},{5,1},{9,5},{13... | collective-permute-start | bytes 147464 | tf_op jit(solution)/shard_map/ppermute | solution.py:17
  31.0 10.8 %copy-start.5 = (bf16[384,96]{0,1:T(8,128)(2,1)S(1)}, bf16[384,96]{0,1:T(8,128)(2,1)}, u32[]{:S(2)}) copy-start(bf16[384,96]{0,1:T(8,128)(2,1)} %param.11) | copy-start | bytes 221188
  41.8 0.6 copy-start.11
  41.8 0.6 copy-start.12
  56.6 26.5 %copy-start.9 = (s32[1,2,64]{2,1,0:T(2,128)S(1)}, s32[1,2,64]{2,1,0:T(2,128)}, u32[]{:S(2)}) copy-start(s32[1,2,64]{2,1,0:T(2,128)} %param.15) | copy-start | bytes 1540
  56.6 26.6 %copy-start.1 = (bf16[4096,96]{1,0:T(8,128)(2,1)S(1)}, bf16[4096,96]{1,0:T(8,128)(2,1)}, u32[]{:S(2)}) copy-start(bf16[4096,96]{1,0:T(8,128)(2,1)} %gather_fusion.3) | copy-start | bytes 2359300
  83.1 97.9 %all-reduce.3.cloned.1.call-start = ((), (), s32[]{:S(2)}) async-start(), calls=%async_computation.2 | async-start | bytes 983040 | tf_op jit(solution)/shard_map/psum | solution.py:77
  107.4 14.4 %copy-start.10 = (bf16[256,468]{0,1:T(8,128)(2,1)S(1)}, bf16[256,468]{0,1:T(8,128)(2,1)}, u32[]{:S(2)}) copy-start(bf16[256,468]{0,1:T(8,128)(2,1)} %param.9) | copy-start | bytes 718852
  111.1 9.4 %collective-permute-start.3 = (f32[1,64,96]{2,1,0:T(8,128)S(1)}, f32[1,64,96]{2,1,0:T(8,128)S(1)}, u32[]{:S(2)}, u32[]{:S(2)}) collective-permute-start(f32[1,64,96]{2,1,0:T(8,128)S(1)} %bitcast.30), channel_id=1, source_target_pairs={{4,0},{8,4},{12,8},{16,12},{20,16},{24,20},{28,24},{5,1},{9,5},{13... | collective-permute-start | bytes 73736 | tf_op jit(solution)/shard_map/ppermute | solution.py:17
  112.4 8.1 %collective-permute-start.2 = (f32[1,64,96]{2,1,0:T(8,128)S(1)}, f32[1,64,96]{2,1,0:T(8,128)S(1)}, u32[]{:S(2)}, u32[]{:S(2)}) collective-permute-start(f32[1,64,96]{2,1,0:T(8,128)S(1)} %bitcast.29), channel_id=1, source_target_pairs={{0,4},{4,8},{8,12},{12,16},{16,20},{20,24},{24,28},{1,5},{5,9},{9,... | collective-permute-start | bytes 73736 | tf_op jit(solution)/shard_map/ppermute | solution.py:15
Sparse Core Ops, SparseCore 0:
  83.2 26.7 reduce-scatter.3
  123.9 56.9 all-reduce.2
where the time goes:
time: 193 us
  other arithmetic  74.8 us (39%)
  local copies, waits for them, and re-layouts  49.1 us (25%)
  waiting for transfers between devices  33.8 us (18%)
  between operations  14.3 us (7%)
  matrix products  10.4 us (5%)
  starting transfers between devices  10.1 us (5%)
    psum x1, waiting for transfers between devices, on_device(): lax.psum((embed_part, send_part, recv_part), 'band')  33 us
    gather x2, local copies, waits for them, and re-layouts, on_device(): edge_pre = send_proj[edge_source] + recv_proj[edge_receiver]  24.9 us
    scatter-add x1, other arithmetic, on_device(): jax.ops.segment_sum(edge_grad.astype(jnp.float32), edge_source, slot_total)  24.4 us
    scatter-add x1, other arithmetic, on_device(): jax.ops.segment_sum(edge_grad.astype(jnp.float32), edge_receiver, mesh_co...  24.2 us
    scatter-add x1, other arithmetic, on_device(): jax.ops.segment_sum(message.astype(jnp.float32), edge_receiver, mesh_count)  23.4 us
    gather x1, local copies, waits for them, and re-layouts, on_device(): mesh_cot[edge_receiver].astype(jnp.float32) * silu_slope(edge_pre)  15 us
    ppermute x2, starting transfers between devices, extended(): lax.ppermute(tail, axis, [(i, (i + 1) % count) for i in range(ends)])  7.46 us
    unnamed x34, local copies, waits for them, and re-layouts  6.26 us
  transfers between devices with their start and end apart: 6, of which 2 were waited for; matrix products, arithmetic and copies ran while one was open for 41% of the time, Pallas kernels for 0%

commit v1 on v0

v1 whole, which is shorter than its diff:
```python
import functools
import math

import jax
import jax.numpy as jnp
from jax import lax
from jax.experimental import pallas as pl
from jax.experimental.pallas import tpu as pltpu
from jax.sharding import PartitionSpec as P

BF = jnp.bfloat16
F32 = jnp.float32
MESH = pl.DeviceIdType.MESH


def mm(a, b):
    return lax.dot_general(a, b, (((1,), (0,)), ((), ())), preferred_element_type=F32)


def mm_nt(a, b):
    return lax.dot_general(a, b, (((1,), (1,)), ((), ())), preferred_element_type=F32)


def eye(size):
    row = lax.broadcasted_iota(jnp.int32, (size, size), 0)
    col = lax.broadcasted_iota(jnp.int32, (size, size), 1)
    return jnp.where(row == col, 1.0, 0.0).astype(BF)


def sigmoid(v):
    return 0.5 + 0.5 * jnp.tanh(0.5 * v)


def flip(index, bit):
    step = 1 << bit
    return index + step - 2 * step * lax.rem(lax.div(index, step), 2)


def body(
    bands, chans, chunk,
    feat, embed, wsend, wrecv, nodes, cot, send, source, receiver,
    mesh_out, early_out, late_out,
    latent, outgoing, outer, tables, acc, slots_out, returned, back_out, back_in,
    xs1, xr1, snd1, rcv1, fin1, xs2, xr2, snd2, rcv2, fin2,
    row_send, row_recv, ret_send, ret_recv, back_send, back_recv, sum_send, sum_recv,
):
    band = lax.axis_index("band")
    chan = lax.axis_index("chan")
    bits = bands.bit_length() - 1
    width = wsend.shape[1]
    grid = feat.shape[0]
    mesh_count = nodes.shape[0]
    cap = outgoing.shape[0] // 2
    slots = grid + 2 * cap
    half = width // 2
    left = lax.rem(band + bands - 1, bands)
    right = lax.rem(band + 1, bands)
    partners = [flip(band, bit) for bit in range(bits)]
    others = [lax.rem(chan + step, chans) for step in range(1, chans)]

    barrier = pltpu.get_barrier_semaphore()
    for peer in [left, right] + partners[1:]:
        pl.semaphore_signal(barrier, inc=1, device_id=(peer, chan), device_id_type=MESH)
    for peer in others:
        pl.semaphore_signal(barrier, inc=1, device_id=(band, peer), device_id_type=MESH)

    def remote(src, dst, send_sem, recv_sem, to_band, to_chan):
        return pltpu.make_async_remote_copy(
            src_ref=src, dst_ref=dst, send_sem=send_sem, recv_sem=recv_sem,
            device_id=(to_band, to_chan), device_id_type=MESH,
        )

    grid_pre = mm(feat[...], embed[...])
    latent[...] = (grid_pre * sigmoid(grid_pre)).astype(BF)
    own = mm(latent[...], wsend[...]).astype(BF)
    picks = lax.broadcasted_iota(jnp.int32, (grid, 2 * cap), 0) == send[...]
    pick_rows = jnp.transpose(jnp.where(picks, 1.0, 0.0)).astype(BF)
    outgoing[...] = mm(pick_rows, own).astype(BF)
    pl.semaphore_wait(barrier, 2 + (bits - 1) + (chans - 1))
    low, high = pl.ds(0, cap), pl.ds(cap, cap)
    rows = [
        remote(outgoing.at[low], outer.at[high], row_send.at[0], row_recv.at[0], left, chan),
        remote(outgoing.at[high], outer.at[low], row_send.at[1], row_recv.at[1], right, chan),
    ]
    for copy in rows:
        copy.start()

    turn = eye(width)
    tables[:width, :grid] = mm_nt(turn, own).astype(BF)
    tables[:width, slots:] = mm_nt(turn, mm(nodes[...], wrecv[...]).astype(BF)).astype(BF)
    tables[width:, :slots] = jnp.zeros((width, slots), BF)
    tables[width:, slots:] = mm_nt(turn, cot[...]).astype(BF)
    acc[...] = jnp.zeros_like(acc)
    choose = lax.broadcasted_iota(jnp.int32, (width, embed.shape[1]), 1) == (
        lax.broadcasted_iota(jnp.int32, (width, embed.shape[1]), 0) + chan * width
    )
    mine = mm_nt(jnp.where(choose, 1.0, 0.0).astype(BF), embed[...]).astype(BF)
    pre_mine = mm_nt(mine, feat[...])
    gate = sigmoid(pre_mine)
    slope_mine = gate * (1.0 + pre_mine * (1.0 - gate))
    for copy in rows:
        copy.wait()
    tables[:width, grid:slots] = mm_nt(turn, outer[...]).astype(BF)

    def edges(step, carry):
        src = source[pl.ds(step, 1), :]
        rec = receiver[pl.ds(step, 1), :]
        hot = jnp.concatenate(
            [
                jnp.where(lax.broadcasted_iota(jnp.int32, (slots, chunk), 0) == src, 1.0, 0.0),
                jnp.where(lax.broadcasted_iota(jnp.int32, (mesh_count, chunk), 0) == rec, 1.0, 0.0),
            ],
            axis=0,
        ).astype(BF)
        drawn = mm(tables[...], hot)
        pre = drawn[:width]
        gate = sigmoid(pre)
        message = pre * gate
        grad = drawn[width:] * (gate + message * (1.0 - gate))
        acc[...] += mm_nt(jnp.concatenate([message, grad], axis=0).astype(BF), hot)
        return carry

    lax.fori_loop(0, source.shape[0], edges, 0)

    slots_out[...] = mm_nt(eye(2 * cap), acc[width:, grid:slots].astype(BF)).astype(BF)
    backs = [
        remote(slots_out.at[low], returned.at[high], ret_send.at[0], ret_recv.at[0], left, chan),
        remote(slots_out.at[high], returned.at[low], ret_send.at[1], ret_recv.at[1], right, chan),
    ]
    for copy in backs:
        copy.start()
    latents = embed.shape[1]
    xs1[:, :latents] = mm(acc[width:, slots:].astype(BF), nodes[...]).astype(BF)
    mesh_out[...] = mm_nt(eye(mesh_count), acc[:width, slots:].astype(BF)).astype(BF)
    for copy in backs:
        copy.wait()
    ret_t = mm_nt(turn, returned[...]).astype(BF)
    total = (acc[width:, :grid].astype(BF).astype(F32) + mm(ret_t, pick_rows)).astype(BF)

    sums = []
    for at, peer in enumerate(others):
        block = wsend[pl.ds(pl.multiple_of(peer * width, width), width), :]
        back_out[at] = mm(block, total).astype(BF)
        copy = remote(back_out.at[at], back_in.at[at], back_send.at[at], back_recv.at[at], band, peer)
        copy.start()
        sums.append(copy)
    grid_grad = mm(wsend[pl.ds(pl.multiple_of(chan * width, width), width), :], total)
    xs1[:, latents:] = mm(total, latent[...]).astype(BF)

    my_half = pl.ds(pl.multiple_of(lax.rem(band, 2) * half, half), half)
    its_half = pl.ds(pl.multiple_of((1 - lax.rem(band, 2)) * half, half), half)

    def reduction(base, xs, xr, snd, rcv, fin):
        middle = xs.shape[1] // 2
        copy = remote(
            xs.at[its_half], xr, sum_send.at[base], sum_recv.at[base], partners[0], chan
        )
        copy.start()
        yield
        copy.wait()
        value = xs[my_half, :].astype(F32) + xr[...].astype(F32)
        for at in range(bits - 1):
            snd[at] = value.astype(BF)
            pair = []
            for side, bit in enumerate((1 + at, bits - 1 - at)):
                cut = pl.ds(side * middle, middle)
                sem = base + 1 + 2 * at + side
                pair.append(
                    remote(
                        snd.at[at, :, cut], rcv.at[at, :, cut],
                        sum_send.at[sem], sum_recv.at[sem], partners[bit], chan,
                    )
                )
            for copy in pair:
                copy.start()
            yield
            for copy in pair:
                copy.wait()
            value = snd[at].astype(F32) + rcv[at].astype(F32)
        fin[my_half, :] = value
        sem = base + 1 + 2 * (bits - 1)
        copy = remote(
            fin.at[my_half], fin.at[my_half], sum_send.at[sem], sum_recv.at[sem], partners[0], chan
        )
        copy.start()
        yield
        copy.wait()
        yield

    early = reduction(0, xs1, xr1, snd1, rcv1, fin1)
    late = reduction(2 * bits, xs2, xr2, snd2, rcv2, fin2)
    next(early)
    next(early)
    for at, copy in enumerate(sums):
        copy.wait()
        grid_grad = grid_grad + back_in[at].astype(F32)
    pre_grad = (grid_grad * slope_mine).astype(BF)
    inputs = feat.shape[1]
    if inputs < xs2.shape[1]:
        xs2[...] = jnp.zeros_like(xs2)
    xs2[:, :inputs] = mm(pre_grad, feat[...]).astype(BF)
    next(late)
    for _ in range(bits - 1):
        next(early)
        next(late)
    next(early)
    early_out[...] = fin1[...]
    next(late)
    next(late)
    late_out[...] = fin2[...]


def on_device(
    grid_feat, w_embed, w_send, w_recv, mesh_nodes, mesh_cot, send_index, edge_source, edge_receiver
):
    bands = lax.axis_size("band")
    chans = lax.axis_size("chan")
    bits = bands.bit_length() - 1
    grid, inputs = grid_feat.shape
    latents, width = w_send.shape
    mesh_count = mesh_nodes.shape[0]
    cap = send_index.shape[2]
    slots = grid + 2 * cap
    half = width // 2
    chunk = math.gcd(edge_source.shape[0], 1024)
    wide1 = 2 * latents
    wide2 = -(-inputs // 256) * 256
    steps = max(bits - 1, 1)
    vmem = pl.BlockSpec(memory_space=pltpu.VMEM)
    mesh_out, early, late = pl.pallas_call(
        functools.partial(body, bands, chans, chunk),
        out_shape=(
            jax.ShapeDtypeStruct((mesh_count, width), BF),
            jax.ShapeDtypeStruct((width, wide1), F32),
            jax.ShapeDtypeStruct((width, wide2), F32),
        ),
        in_specs=[vmem] * 9,
        out_specs=(vmem,) * 3,
        scratch_shapes=[
            pltpu.VMEM((grid, latents), BF),
            pltpu.VMEM((2 * cap, width), BF),
            pltpu.VMEM((2 * cap, width), BF),
            pltpu.VMEM((2 * width, slots + mesh_count), BF),
            pltpu.VMEM((2 * width, slots + mesh_count), F32),
            pltpu.VMEM((2 * cap, width), BF),
            pltpu.VMEM((2 * cap, width), BF),
            pltpu.VMEM((chans - 1, width, grid), BF),
            pltpu.VMEM((chans - 1, width, grid), BF),
        ]
        + [
            pltpu.VMEM(shape, kind)
            for wide in (wide1, wide2)
            for shape, kind in (
                ((width, wide), BF),
                ((half, wide), BF),
                ((steps, half, wide), BF),
                ((steps, half, wide), BF),
                ((width, wide), F32),
            )
        ]
        + [
            pltpu.SemaphoreType.DMA((count,))
            for count in (2, 2, 2, 2, chans - 1, chans - 1, 4 * bits, 4 * bits)
        ],
        compiler_params=pltpu.CompilerParams(collective_id=0, has_side_effects=True),
    )(
        grid_feat, w_embed, w_send, w_recv, mesh_nodes, mesh_cot,
        send_index.reshape(1, 2 * cap),
        edge_source.reshape(-1, chunk),
        edge_receiver.reshape(-1, chunk),
    )
    return (
        mesh_out,
        late[:, :inputs].T,
        early[:, latents:].T,
        early[:, :latents].T,
    )


def solution(mesh):
    placed = (
        P("band", None),
        P(),
        P(None, "chan"),
        P(None, "chan"),
        P("band", None),
        P("band", "chan"),
        P("band", None, None),
        P("band"),
        P("band"),
    )
    return jax.shard_map(
        on_device,
        mesh=mesh,
        in_specs=placed,
        out_specs=(P("band", "chan"), P(None, "chan"), P(None, "chan"), P(None, "chan")),
        check_vma=False,
    )
```

time: 193 us -> 43.5 us (0.23)
  other arithmetic: 74.8 us -> 0 us
  local copies, waits for them, and re-layouts: 49.1 us -> 11.1 us
  waiting for transfers between devices: 33.8 us -> 0 us
  Pallas kernels: 0 us -> 31.4 us
  between operations: 14.3 us -> 0.66 us
  matrix products: 10.4 us -> 0 us
  starting transfers between devices: 10.1 us -> 0 us
    scatter-add x4 -> x0, other arithmetic: 73.2 us -> none  [the longest x1 24.4 us: on_device(): jax.ops.segment_sum(edge_grad.astype(jnp.float32), edge_source, slot_total)]
    gather x4 -> x0, local copies, waits for them, and re-layouts: 40.8 us -> none  [the longest x2 24.9 us: on_device(): edge_pre = send_proj[edge_source] + recv_proj[edge_receiver]]
    psum x1 -> x0, waiting for transfers between devices: 33 us -> none  [on_device(): lax.psum((embed_part, send_part, recv_part), 'band')]
    pallas_call x0 -> x1, Pallas kernels: none -> 31.4 us  [on_device(): pl.pallas_call(functools.partial(body, bands, chans, chunk), out_shape=(j...]
    ppermute x4 -> x0, starting transfers between devices: 10.1 us -> none  [the longest x2 7.46 us: extended(): lax.ppermute(tail, axis, [(i, (i + 1) % count) for i in range(ends)])]
    dot_general x6 -> x0, matrix products: 8.33 us -> none  [the longest x1 2.03 us: on_device(): grid_pre = jnp.dot(grid_feat, w_embed, preferred_element_type=jnp.float32)]
    reshape x0 -> x3, local copies, waits for them, and re-layouts: none -> 4.08 us  [the longest x1 1.37 us: on_device(): edge_receiver.reshape(-1, chunk)]
    transpose x0 -> x2, local copies, waits for them, and re-layouts: none -> 2.34 us  [the longest x1 1.62 us: on_device(): late[:, :inputs]]
  transfers between devices with their start and end apart: 6 -> 0, of which waited for: 2 -> 0; matrix products, arithmetic and copies ran while one was open for 41% -> 0% of each run, Pallas kernels for 0% -> 0%
where the time goes in v1:
time: 43.5 us; the launch traced here: 43.2 us
  Pallas kernels  31.4 us (72%)
  local copies, waits for them, and re-layouts  11.1 us (26%)
  between operations  0.66 us (2%)
    pallas_call x1, Pallas kernels, on_device(): pl.pallas_call(functools.partial(body, bands, chans, chunk), out_shape=(j...  31.4 us
    unnamed x15, local copies, waits for them, and re-layouts  4.71 us
    transpose x1, local copies, waits for them, and re-layouts, on_device(): late[:, :inputs]  1.62 us
    reshape x1, local copies, waits for them, and re-layouts, on_device(): edge_receiver.reshape(-1, chunk)  1.37 us
    reshape x1, local copies, waits for them, and re-layouts, on_device(): edge_source.reshape(-1, chunk)  1.37 us
    reshape x1, local copies, waits for them, and re-layouts, on_device(): send_index.reshape(1, 2 * cap)  1.34 us

profile of v1, /device:TPU:0, one launch (start us, length us, event | category | flops | bytes accessed | tf_op | source)
XLA Modules:
  0.0 43.2 jit_solution(14331004899761998989)
XLA Ops:
  0.6 0.0 copy-start.4
  0.6 1.3 %reshape.17.send = s32[1,128]{1,0:T(1,128)} reshape(s32[1,2,64]{2,1,0:T(2,128)} %param.15) | data formatting | bytes 1024 | tf_op jit(solution)/shard_map/reshape | solution.py:268
  2.0 0.0 copy-start.2
  2.0 0.0 copy-start.3
  2.0 1.4 %reshape.18.source = s32[4,1024]{1,0:T(4,128)} reshape(s32[4096]{0:T(1024)} %param.16) | data formatting | bytes 32768 | tf_op jit(solution)/shard_map/reshape | solution.py:269
  3.4 0.0 copy-start.1
  3.4 1.4 %reshape.19.receiver = s32[4,1024]{1,0:T(4,128)} reshape(s32[4096]{0:T(1024)} %param.17) | data formatting | bytes 32768 | tf_op jit(solution)/shard_map/reshape | solution.py:270
  4.7 0.0 copy-done.4
  4.7 0.7 %copy.16.cot = bf16[256,96]{1,0:T(8,128)(2,1)} copy(bf16[256,96]{0,1:T(8,128)(2,1)S(1)} %copy-done.4) | data formatting | bytes 98304 | tf_op args[5]
  5.5 0.0 copy-done.2
  5.5 0.8 %copy.14.wsend = bf16[384,96]{1,0:T(8,128)(2,1)} copy(bf16[384,96]{0,1:T(8,128)(2,1)S(1)} %copy-done.2) | data formatting | bytes 147456 | tf_op args[2]
  6.2 0.0 copy-done.3
  6.2 0.8 %copy.15.wrecv = bf16[384,96]{1,0:T(8,128)(2,1)} copy(bf16[384,96]{0,1:T(8,128)(2,1)S(1)} %copy-done.3) | data formatting | bytes 147456 | tf_op args[3]
  7.0 0.0 copy-done.1
  7.0 0.9 %copy.13.feat = bf16[256,468]{1,0:T(8,128)(2,1)} copy(bf16[256,468]{0,1:T(8,128)(2,1)S(1)} %copy-done.1) | data formatting | bytes 479232 | tf_op args[0]
  7.8 31.4 %shard_map.120 = (bf16[256,96]{1,0:T(8,128)(2,1)}, f32[96,768]{1,0:T(8,128)}, f32[96,512]{1,0:T(8,128)}) custom-call(bf16[256,468]{1,0:T(8,128)(2,1)} %copy.13.feat, bf16[468,384]{1,0:T(8,128)(2,1)} %embed.1, bf16[384,96]{1,0:T(8,128)(2,1)} %copy.14.wsend, bf16[384,96]{1,0:T(8,128)(2,1)} %copy.15.wrecv, bf16[256,384]{1,0:T(8,128)(2,1)} %nodes.1, ...), custom_call_target="tpu_custom_call" | custom-call | tf_op jit(solution)/shard_map/pallas_call | solution.py:230
  39.2 0.0 copy-start
  39.2 1.6 %copy.17 = bf16[256,96]{0,1:T(8,128)(2,1)} copy(bf16[256,96]{1,0:T(8,128)(2,1)} %get-tuple-element.10) | data formatting | bytes 98304
  40.8 1.6 %slice_bitcast_fusion = f32[468,96]{0,1:T(8,128)} fusion(f32[96,512]{1,0:T(8,128)} %get-tuple-element.8), kind=kLoop, calls=%fused_computation | loop fusion | bytes 359424 | tf_op jit(solution)/shard_map/transpose | solution.py:274
  42.5 0.0 copy-done
  42.5 0.7 %slice_bitcast_fusion.1 = (f32[384,96]{0,1:T(8,128)}, f32[384,96]{0,1:T(8,128)}) fusion(f32[96,768]{1,0:T(8,128)S(1)} %copy-done), kind=kLoop, calls=%fused_computation.1 | loop fusion | bytes 589824 | tf_op jit(solution)/shard_map/transpose | solution.py:276
Async XLA Ops:
  0.6 4.1 %copy-start.4 = (bf16[256,96]{0,1:T(8,128)(2,1)S(1)}, bf16[256,96]{0,1:T(8,128)(2,1)}, u32[]{:S(2)}) copy-start(bf16[256,96]{0,1:T(8,128)(2,1)} %param.14) | copy-start | bytes 147460
  2.0 3.5 %copy-start.2 = (bf16[384,96]{0,1:T(8,128)(2,1)S(1)}, bf16[384,96]{0,1:T(8,128)(2,1)}, u32[]{:S(2)}) copy-start(bf16[384,96]{0,1:T(8,128)(2,1)} %param.11) | copy-start | bytes 221188
  2.0 4.2 %copy-start.3 = (bf16[384,96]{0,1:T(8,128)(2,1)S(1)}, bf16[384,96]{0,1:T(8,128)(2,1)}, u32[]{:S(2)}) copy-start(bf16[384,96]{0,1:T(8,128)(2,1)} %param.12) | copy-start | bytes 221188
  3.4 3.6 %copy-start.1 = (bf16[256,468]{0,1:T(8,128)(2,1)S(1)}, bf16[256,468]{0,1:T(8,128)(2,1)}, u32[]{:S(2)}) copy-start(bf16[256,468]{0,1:T(8,128)(2,1)} %param.9) | copy-start | bytes 718852
  39.2 3.2 %copy-start = (f32[96,768]{1,0:T(8,128)S(1)}, f32[96,768]{1,0:T(8,128)}, u32[]{:S(2)}) copy-start(f32[96,768]{1,0:T(8,128)} %get-tuple-element.9) | copy-start | bytes 884740

commit v2 on v1

--- a/solution.py
+++ b/solution.py
@@ -17,6 +17,10 @@
     return lax.dot_general(a, b, (((1,), (0,)), ((), ())), preferred_element_type=F32)
 
 
+def mm_tn(a, b):
+    return lax.dot_general(a, b, (((0,), (0,)), ((), ())), preferred_element_type=F32)
+
+
 def mm_nt(a, b):
     return lax.dot_general(a, b, (((1,), (1,)), ((), ())), preferred_element_type=F32)
 
@@ -39,16 +43,16 @@
 def body(
     bands, chans, chunk,
     feat, embed, wsend, wrecv, nodes, cot, send, source, receiver,
-    mesh_out, early_out, late_out,
-    latent, outgoing, outer, tables, acc, slots_out, returned, back_out, back_in,
+    mesh_out, late_out, send_out, recv_out,
+    latent, back_weight, outgoing, outer, tables, acc, slots_out, returned, back_out, back_in,
     xs1, xr1, snd1, rcv1, fin1, xs2, xr2, snd2, rcv2, fin2,
     row_send, row_recv, ret_send, ret_recv, back_send, back_recv, sum_send, sum_recv,
 ):
     band = lax.axis_index("band")
     chan = lax.axis_index("chan")
     bits = bands.bit_length() - 1
-    width = wsend.shape[1]
-    grid = feat.shape[0]
+    width = wsend.shape[0]
+    grid = feat.shape[1]
     mesh_count = nodes.shape[0]
     cap = outgoing.shape[0] // 2
     slots = grid + 2 * cap
@@ -70,12 +74,14 @@
             device_id=(to_band, to_chan), device_id_type=MESH,
         )
 
-    grid_pre = mm(feat[...], embed[...])
+    grid_pre = mm_tn(feat[...], embed[...])
     latent[...] = (grid_pre * sigmoid(grid_pre)).astype(BF)
-    own = mm(latent[...], wsend[...]).astype(BF)
-    picks = lax.broadcasted_iota(jnp.int32, (grid, 2 * cap), 0) == send[...]
+    own = mm_nt(wsend[...], latent[...]).astype(BF)
+    picks = lax.broadcasted_iota(jnp.int32, (grid, 2 * cap), 0) == jnp.concatenate(
+        [send[0, 0:1, :], send[0, 1:2, :]], axis=1
+    )
     pick_rows = jnp.transpose(jnp.where(picks, 1.0, 0.0)).astype(BF)
-    outgoing[...] = mm(pick_rows, own).astype(BF)
+    outgoing[...] = mm_nt(pick_rows, own).astype(BF)
     pl.semaphore_wait(barrier, 2 + (bits - 1) + (chans - 1))
     low, high = pl.ds(0, cap), pl.ds(cap, cap)
     rows = [
@@ -86,16 +92,17 @@
         copy.start()
 
     turn = eye(width)
-    tables[:width, :grid] = mm_nt(turn, own).astype(BF)
-    tables[:width, slots:] = mm_nt(turn, mm(nodes[...], wrecv[...]).astype(BF)).astype(BF)
+    tables[:width, :grid] = own
+    tables[:width, slots:] = mm_nt(wrecv[...], nodes[...]).astype(BF)
     tables[width:, :slots] = jnp.zeros((width, slots), BF)
-    tables[width:, slots:] = mm_nt(turn, cot[...]).astype(BF)
+    tables[width:, slots:] = cot[...]
     acc[...] = jnp.zeros_like(acc)
+    back_weight[...] = mm_nt(eye(wsend.shape[1]), wsend[...]).astype(BF)
     choose = lax.broadcasted_iota(jnp.int32, (width, embed.shape[1]), 1) == (
         lax.broadcasted_iota(jnp.int32, (width, embed.shape[1]), 0) + chan * width
     )
     mine = mm_nt(jnp.where(choose, 1.0, 0.0).astype(BF), embed[...]).astype(BF)
-    pre_mine = mm_nt(mine, feat[...])
+    pre_mine = mm(mine, feat[...])
     gate = sigmoid(pre_mine)
     slope_mine = gate * (1.0 + pre_mine * (1.0 - gate))
     for copy in rows:
@@ -103,8 +110,8 @@
     tables[:width, grid:slots] = mm_nt(turn, outer[...]).astype(BF)
 
     def edges(step, carry):
-        src = source[pl.ds(step, 1), :]
-        rec = receiver[pl.ds(step, 1), :]
+        src = source[pl.ds(pl.multiple_of(step * chunk, chunk), chunk)].reshape(1, chunk)
+        rec = receiver[pl.ds(pl.multiple_of(step * chunk, chunk), chunk)].reshape(1, chunk)
         hot = jnp.concatenate(
             [
                 jnp.where(lax.broadcasted_iota(jnp.int32, (slots, chunk), 0) == src, 1.0, 0.0),
@@ -120,7 +127,7 @@
         acc[...] += mm_nt(jnp.concatenate([message, grad], axis=0).astype(BF), hot)
         return carry
 
-    lax.fori_loop(0, source.shape[0], edges, 0)
+    lax.fori_loop(0, source.shape[0] // chunk, edges, 0)
 
     slots_out[...] = mm_nt(eye(2 * cap), acc[width:, grid:slots].astype(BF)).astype(BF)
     backs = [
@@ -131,7 +138,7 @@
         copy.start()
     latents = embed.shape[1]
     xs1[:, :latents] = mm(acc[width:, slots:].astype(BF), nodes[...]).astype(BF)
-    mesh_out[...] = mm_nt(eye(mesh_count), acc[:width, slots:].astype(BF)).astype(BF)
+    mesh_out[...] = acc[:width, slots:].astype(BF)
     for copy in backs:
         copy.wait()
     ret_t = mm_nt(turn, returned[...]).astype(BF)
@@ -139,12 +146,12 @@
 
     sums = []
     for at, peer in enumerate(others):
-        block = wsend[pl.ds(pl.multiple_of(peer * width, width), width), :]
+        block = back_weight[pl.ds(pl.multiple_of(peer * width, width), width), :]
         back_out[at] = mm(block, total).astype(BF)
         copy = remote(back_out.at[at], back_in.at[at], back_send.at[at], back_recv.at[at], band, peer)
         copy.start()
         sums.append(copy)
-    grid_grad = mm(wsend[pl.ds(pl.multiple_of(chan * width, width), width), :], total)
+    grid_grad = mm(back_weight[pl.ds(pl.multiple_of(chan * width, width), width), :], total)
     xs1[:, latents:] = mm(total, latent[...]).astype(BF)
 
     my_half = pl.ds(pl.multiple_of(lax.rem(band, 2) * half, half), half)
@@ -195,19 +202,20 @@
         copy.wait()
         grid_grad = grid_grad + back_in[at].astype(F32)
     pre_grad = (grid_grad * slope_mine).astype(BF)
-    inputs = feat.shape[1]
+    inputs = feat.shape[0]
     if inputs < xs2.shape[1]:
         xs2[...] = jnp.zeros_like(xs2)
-    xs2[:, :inputs] = mm(pre_grad, feat[...]).astype(BF)
+    xs2[:, :inputs] = mm_nt(pre_grad, feat[...]).astype(BF)
     next(late)
     for _ in range(bits - 1):
         next(early)
         next(late)
     next(early)
-    early_out[...] = fin1[...]
+    recv_out[...] = fin1[:, :latents]
+    send_out[...] = fin1[:, latents:]
     next(late)
     next(late)
-    late_out[...] = fin2[...]
+    late_out[...] = fin2[:, :inputs]
 
 
 def on_device(
@@ -227,17 +235,19 @@
     wide2 = -(-inputs // 256) * 256
     steps = max(bits - 1, 1)
     vmem = pl.BlockSpec(memory_space=pltpu.VMEM)
-    mesh_out, early, late = pl.pallas_call(
+    outs = pl.pallas_call(
         functools.partial(body, bands, chans, chunk),
         out_shape=(
-            jax.ShapeDtypeStruct((mesh_count, width), BF),
-            jax.ShapeDtypeStruct((width, wide1), F32),
-            jax.ShapeDtypeStruct((width, wide2), F32),
+            jax.ShapeDtypeStruct((width, mesh_count), BF),
+            jax.ShapeDtypeStruct((width, inputs), F32),
+            jax.ShapeDtypeStruct((width, latents), F32),
+            jax.ShapeDtypeStruct((width, latents), F32),
         ),
         in_specs=[vmem] * 9,
-        out_specs=(vmem,) * 3,
+        out_specs=(vmem,) * 4,
         scratch_shapes=[
             pltpu.VMEM((grid, latents), BF),
+            pltpu.VMEM((latents, width), BF),
             pltpu.VMEM((2 * cap, width), BF),
             pltpu.VMEM((2 * cap, width), BF),
             pltpu.VMEM((2 * width, slots + mesh_count), BF),
@@ -264,17 +274,10 @@
         ],
         compiler_params=pltpu.CompilerParams(collective_id=0, has_side_effects=True),
     )(
-        grid_feat, w_embed, w_send, w_recv, mesh_nodes, mesh_cot,
-        send_index.reshape(1, 2 * cap),
-        edge_source.reshape(-1, chunk),
-        edge_receiver.reshape(-1, chunk),
-    )
-    return (
-        mesh_out,
-        late[:, :inputs].T,
-        early[:, latents:].T,
-        early[:, :latents].T,
-    )
+        grid_feat.T, w_embed, w_send.T, w_recv.T, mesh_nodes, mesh_cot.T,
+        send_index, edge_source, edge_receiver,
+    )
+    return tuple(out.T for out in outs)
 
 
 def solution(mesh):

time: 43.5 us -> 37 us (0.85)
  local copies, waits for them, and re-layouts: 11.1 us -> 4.7 us
    reshape x3 -> x0, local copies, waits for them, and re-layouts: 4.08 us -> none  [the longest x1 1.37 us: on_device(): edge_receiver.reshape(-1, chunk)]
    transpose x2 -> x0, local copies, waits for them, and re-layouts: 2.34 us -> none  [the longest x1 1.62 us: on_device(): late[:, :inputs]]
    unnamed x15 -> x8, local copies, waits for them, and re-layouts: 4.71 us -> 4.7 us
where the time goes in v2:
time: 37 us; the launch traced here: 36.7 us
  Pallas kernels  31.4 us (85%)
  local copies, waits for them, and re-layouts  4.7 us (13%)
  between operations  0.65 us (2%)
    pallas_call x1, Pallas kernels, on_device(): pl.pallas_call(functools.partial(body, bands, chans, chunk), out_shape=(j...  31.4 us
    unnamed x8, local copies, waits for them, and re-layouts  4.7 us

profile of v2, /device:TPU:0, one launch (start us, length us, event | category | flops | bytes accessed | tf_op | source)
XLA Modules:
  0.0 36.7 jit_solution(14217364683765597749)
XLA Ops:
  0.6 31.4 %shard_map.120 = (bf16[96,256]{1,0:T(8,128)(2,1)}, f32[96,468]{1,0:T(8,128)}, f32[96,384]{1,0:T(8,128)}, f32[96,384]{1,0:T(8,128)}) custom-call(bf16[468,256]{1,0:T(8,128)(2,1)} %bitcast.8, bf16[468,384]{1,0:T(8,128)(2,1)} %embed.1, bf16[96,384]{1,0:T(8,128)(2,1)} %bitcast.12, bf16[96,384]{1,0:T(8,128)(2,1)} %bitcast.13, bf16[256,384]{1,0:T(8,128)(2,1)} %nodes.1, ...), custom_call_target="tpu_custom_call" | custom-call | tf_op jit(solution)/shard_map/pallas_call | solution.py:238
  32.0 1.4 %copy.17 = bf16[256,96]{0,1:T(8,128)(2,1)} copy(bf16[256,96]{0,1:T(8,128)(2,1)} %bitcast.15) | data formatting | bytes 98304
  33.5 0.0 copy-start.1
  33.5 1.7 %copy.18 = f32[468,96]{0,1:T(8,128)} copy(f32[468,96]{0,1:T(8,128)} %bitcast.9) | data formatting | bytes 359424
  35.1 0.0 copy-done.1
  35.1 0.0 copy-start
  35.1 0.7 %copy.19 = f32[384,96]{0,1:T(8,128)} copy(f32[384,96]{0,1:T(8,128)S(1)} %bitcast.11) | data formatting | bytes 294912
  35.8 0.3 copy-done
  36.1 0.7 %copy.20 = f32[384,96]{0,1:T(8,128)} copy(f32[384,96]{0,1:T(8,128)S(1)} %bitcast.10) | data formatting | bytes 294912
Async XLA Ops:
  33.5 1.7 %copy-start.1 = (f32[96,384]{1,0:T(8,128)S(1)}, f32[96,384]{1,0:T(8,128)}, u32[]{:S(2)}) copy-start(f32[96,384]{1,0:T(8,128)} %get-tuple-element.10) | copy-start | bytes 442372
  35.1 1.0 %copy-start = (f32[96,384]{1,0:T(8,128)S(1)}, f32[96,384]{1,0:T(8,128)}, u32[]{:S(2)}) copy-start(f32[96,384]{1,0:T(8,128)} %get-tuple-element.11) | copy-start | bytes 442372

commit v3 on v2

--- a/solution.py
+++ b/solution.py
@@ -42,8 +42,9 @@
 
 def body(
     bands, chans, chunk,
-    feat, embed, wsend, wrecv, nodes, cot, send, source, receiver,
+    feat_in, embed_in, wsend_in, wrecv_in, nodes_in, cot_in, send_in, source_in, receiver_in,
     mesh_out, late_out, send_out, recv_out,
+    feat, embed, wsend, wrecv, nodes, cot, send, source, receiver, loads,
     latent, back_weight, outgoing, outer, tables, acc, slots_out, returned, back_out, back_in,
     xs1, xr1, snd1, rcv1, fin1, xs2, xr2, snd2, rcv2, fin2,
     row_send, row_recv, ret_send, ret_recv, back_send, back_recv, sum_send, sum_recv,
@@ -68,19 +69,34 @@
     for peer in others:
         pl.semaphore_signal(barrier, inc=1, device_id=(band, peer), device_id_type=MESH)
 
+    pulls = {}
+    for at, (name, src, dst) in enumerate(
+        (
+            ("feat", feat_in, feat), ("embed", embed_in, embed), ("send", send_in, send),
+            ("wsend", wsend_in, wsend), ("nodes", nodes_in, nodes), ("wrecv", wrecv_in, wrecv),
+            ("cot", cot_in, cot), ("source", source_in, source), ("receiver", receiver_in, receiver),
+        )
+    ):
+        pulls[name] = pltpu.make_async_copy(src, dst, loads.at[at])
+        pulls[name].start()
+
     def remote(src, dst, send_sem, recv_sem, to_band, to_chan):
         return pltpu.make_async_remote_copy(
             src_ref=src, dst_ref=dst, send_sem=send_sem, recv_sem=recv_sem,
             device_id=(to_band, to_chan), device_id_type=MESH,
         )
 
+    pulls["send"].wait()
+    picks = lax.broadcasted_iota(jnp.int32, (grid, 2 * cap), 0) == jnp.concatenate(
+        [send[0, 0:1, :], send[0, 1:2, :]], axis=1
+    )
+    pick_rows = jnp.transpose(jnp.where(picks, 1.0, 0.0)).astype(BF)
+    pulls["feat"].wait()
+    pulls["embed"].wait()
     grid_pre = mm_tn(feat[...], embed[...])
     latent[...] = (grid_pre * sigmoid(grid_pre)).astype(BF)
+    pulls["wsend"].wait()
     own = mm_nt(wsend[...], latent[...]).astype(BF)
-    picks = lax.broadcasted_iota(jnp.int32, (grid, 2 * cap), 0) == jnp.concatenate(
-        [send[0, 0:1, :], send[0, 1:2, :]], axis=1
-    )
-    pick_rows = jnp.transpose(jnp.where(picks, 1.0, 0.0)).astype(BF)
     outgoing[...] = mm_nt(pick_rows, own).astype(BF)
     pl.semaphore_wait(barrier, 2 + (bits - 1) + (chans - 1))
     low, high = pl.ds(0, cap), pl.ds(cap, cap)
@@ -92,6 +108,8 @@
         copy.start()
 
     turn = eye(width)
+    for name in ("nodes", "wrecv", "cot", "source", "receiver"):
+        pulls[name].wait()
     tables[:width, :grid] = own
     tables[:width, slots:] = mm_nt(wrecv[...], nodes[...]).astype(BF)
     tables[width:, :slots] = jnp.zeros((width, slots), BF)
@@ -196,8 +214,8 @@
 
     early = reduction(0, xs1, xr1, snd1, rcv1, fin1)
     late = reduction(2 * bits, xs2, xr2, snd2, rcv2, fin2)
-    next(early)
-    next(early)
+    for _ in range(bits):
+        next(early)
     for at, copy in enumerate(sums):
         copy.wait()
         grid_grad = grid_grad + back_in[at].astype(F32)
@@ -207,15 +225,25 @@
         xs2[...] = jnp.zeros_like(xs2)
     xs2[:, :inputs] = mm_nt(pre_grad, feat[...]).astype(BF)
     next(late)
-    for _ in range(bits - 1):
-        next(early)
-        next(late)
+    next(early)
+    next(late)
     next(early)
     recv_out[...] = fin1[:, :latents]
     send_out[...] = fin1[:, latents:]
-    next(late)
-    next(late)
+    for _ in range(bits):
+        next(late)
     late_out[...] = fin2[:, :inputs]
+
+
+def place(count, *refs):
+    sems = refs[2 * count]
+    copies = [
+        pltpu.make_async_copy(refs[at], refs[count + at], sems.at[at]) for at in range(count)
+    ]
+    for copy in copies:
+        copy.start()
+    for copy in copies:
+        copy.wait()
 
 
 def on_device(
@@ -235,17 +263,25 @@
     wide2 = -(-inputs // 256) * 256
     steps = max(bits - 1, 1)
     vmem = pl.BlockSpec(memory_space=pltpu.VMEM)
+    arrays = (
+        grid_feat.T, w_embed, w_send.T, w_recv.T, mesh_nodes, mesh_cot.T,
+        send_index, edge_source, edge_receiver,
+    )
     outs = pl.pallas_call(
         functools.partial(body, bands, chans, chunk),
         out_shape=(
-            jax.ShapeDtypeStruct((width, mesh_count), BF),
-            jax.ShapeDtypeStruct((width, inputs), F32),
-            jax.ShapeDtypeStruct((width, latents), F32),
-            jax.ShapeDtypeStruct((width, latents), F32),
+            pltpu.VMEM((width, mesh_count), BF),
+            pltpu.VMEM((width, inputs), F32),
+            pltpu.VMEM((width, latents), F32),
+            pltpu.VMEM((width, latents), F32),
         ),
-        in_specs=[vmem] * 9,
+        in_specs=[pl.BlockSpec(memory_space=pl.ANY)] * 9,
         out_specs=(vmem,) * 4,
         scratch_shapes=[
+            pltpu.VMEM(array.shape, array.dtype) for array in arrays
+        ]
+        + [
+            pltpu.SemaphoreType.DMA((9,)),
             pltpu.VMEM((grid, latents), BF),
             pltpu.VMEM((latents, width), BF),
             pltpu.VMEM((2 * cap, width), BF),
@@ -273,11 +309,16 @@
             for count in (2, 2, 2, 2, chans - 1, chans - 1, 4 * bits, 4 * bits)
         ],
         compiler_params=pltpu.CompilerParams(collective_id=0, has_side_effects=True),
-    )(
-        grid_feat.T, w_embed, w_send.T, w_recv.T, mesh_nodes, mesh_cot.T,
-        send_index, edge_source, edge_receiver,
-    )
-    return tuple(out.T for out in outs)
+    )(*arrays)
+    anywhere = pl.BlockSpec(memory_space=pl.ANY)
+    placed = pl.pallas_call(
+        functools.partial(place, len(outs)),
+        out_shape=tuple(jax.ShapeDtypeStruct(out.shape, out.dtype) for out in outs),
+        in_specs=[vmem] * len(outs),
+        out_specs=(anywhere,) * len(outs),
+        scratch_shapes=[pltpu.SemaphoreType.DMA((len(outs),))],
+    )(*(pltpu.with_memory_space_constraint(out, pltpu.VMEM) for out in outs))
+    return tuple(out.T for out in placed)
 
 
 def solution(mesh):

time: 37 us -> 32.2 us (0.87)
  local copies, waits for them, and re-layouts: 4.7 us -> 0 us
    unnamed x8 -> x0, local copies, waits for them, and re-layouts: 4.7 us -> none
    pallas_call x1 -> x2, Pallas kernels: 31.4 us -> 31.4 us  [the longest x1 30.6 us: on_device(): pl.pallas_call(functools.partial(body, bands, chans, chunk), out_shape=(p...]
where the time goes in v3:
time: 32.2 us; the launch traced here: 32.1 us
  Pallas kernels  31.4 us (98%)
  between operations  0.64 us (2%)
    pallas_call x1, Pallas kernels, on_device(): pl.pallas_call(functools.partial(body, bands, chans, chunk), out_shape=(p...  30.6 us
    pallas_call x1, Pallas kernels, on_device(): pl.pallas_call(functools.partial(place, len(outs)), out_shape=tuple((jax....  0.83 us

profile of v3, /device:TPU:0, one launch (start us, length us, event | category | flops | bytes accessed | tf_op | source)
XLA Modules:
  0.0 32.1 jit_solution(12390823152685397151)
XLA Ops:
  0.6 30.6 %shard_map.120 = (bf16[96,256]{1,0:T(8,128)(2,1)S(1)}, f32[96,468]{1,0:T(8,128)S(1)}, f32[96,384]{1,0:T(8,128)S(1)}, f32[96,384]{1,0:T(8,128)S(1)}) custom-call(bf16[468,256]{1,0:T(8,128)(2,1)} %bitcast.8, bf16[468,384]{1,0:T(8,128)(2,1)} %embed_in.1, bf16[96,384]{1,0:T(8,128)(2,1)} %bitcast.9, bf16[96,384]{1,0:T(8,128)(2,1)} %bitcast.10, ...), custom_call_target="tpu_custom_call" | custom-call | tf_op jit(solution)/shard_map/pallas_call | solution.py:270
  31.2 0.8 %shard_map.121 = (bf16[96,256]{1,0:T(8,128)(2,1)}, f32[96,468]{1,0:T(8,128)}, f32[96,384]{1,0:T(8,128)}, f32[96,384]{1,0:T(8,128)}) custom-call(bf16[96,256]{1,0:T(8,128)(2,1)S(1)} %get-tuple-element.12.refs_0_, f32[96,468]{1,0:T(8,128)S(1)} %get-tuple-element.13.refs_1_, f32[96,384]{1,0:T(8,128)S(1)} %get-tuple-element.14.refs_2_, ...), custom_call_target="tpu_custom_call" | custom-call | tf_op jit(solution)/shard_map/pallas_call | solution.py:314

commit v4 on v3

--- a/solution.py
+++ b/solution.py
@@ -45,7 +45,7 @@
     feat_in, embed_in, wsend_in, wrecv_in, nodes_in, cot_in, send_in, source_in, receiver_in,
     mesh_out, late_out, send_out, recv_out,
     feat, embed, wsend, wrecv, nodes, cot, send, source, receiver, loads,
-    latent, back_weight, outgoing, outer, tables, acc, slots_out, returned, back_out, back_in,
+    latent, back_weight, outgoing, outer, tables, acc, hot_recv, drawn_recv, slots_out, returned, back_out, back_in,
     xs1, xr1, snd1, rcv1, fin1, xs2, xr2, snd2, rcv2, fin2,
     row_send, row_recv, ret_send, ret_recv, back_send, back_recv, sum_send, sum_recv,
 ):
@@ -112,7 +112,6 @@
         pulls[name].wait()
     tables[:width, :grid] = own
     tables[:width, slots:] = mm_nt(wrecv[...], nodes[...]).astype(BF)
-    tables[width:, :slots] = jnp.zeros((width, slots), BF)
     tables[width:, slots:] = cot[...]
     acc[...] = jnp.zeros_like(acc)
     back_weight[...] = mm_nt(eye(wsend.shape[1]), wsend[...]).astype(BF)
@@ -123,29 +122,36 @@
     pre_mine = mm(mine, feat[...])
     gate = sigmoid(pre_mine)
     slope_mine = gate * (1.0 + pre_mine * (1.0 - gate))
+
+    def one_hot(index, count, step):
+        at = index[pl.ds(pl.multiple_of(step * chunk, chunk), chunk)].reshape(1, chunk)
+        hit = lax.broadcasted_iota(jnp.int32, (count, chunk), 0) == at
+        return jnp.where(hit, 1.0, 0.0).astype(BF)
+
+    def receivers(step, carry):
+        hot = one_hot(receiver, mesh_count, step)
+        hot_recv[step] = hot
+        drawn_recv[step] = mm(tables[:, slots:], hot)
+        return carry
+
+    steps = source.shape[0] // chunk
+    lax.fori_loop(0, steps, receivers, 0)
     for copy in rows:
         copy.wait()
     tables[:width, grid:slots] = mm_nt(turn, outer[...]).astype(BF)
 
     def edges(step, carry):
-        src = source[pl.ds(pl.multiple_of(step * chunk, chunk), chunk)].reshape(1, chunk)
-        rec = receiver[pl.ds(pl.multiple_of(step * chunk, chunk), chunk)].reshape(1, chunk)
-        hot = jnp.concatenate(
-            [
-                jnp.where(lax.broadcasted_iota(jnp.int32, (slots, chunk), 0) == src, 1.0, 0.0),
-                jnp.where(lax.broadcasted_iota(jnp.int32, (mesh_count, chunk), 0) == rec, 1.0, 0.0),
-            ],
-            axis=0,
-        ).astype(BF)
-        drawn = mm(tables[...], hot)
-        pre = drawn[:width]
+        hot = one_hot(source, slots, step)
+        pre = mm(tables[:width, :slots], hot) + drawn_recv[step, :width, :]
         gate = sigmoid(pre)
         message = pre * gate
-        grad = drawn[width:] * (gate + message * (1.0 - gate))
-        acc[...] += mm_nt(jnp.concatenate([message, grad], axis=0).astype(BF), hot)
+        grad = drawn_recv[step, width:, :] * (gate + message * (1.0 - gate))
+        both = jnp.concatenate([message, grad], axis=0).astype(BF)
+        acc[width:, :slots] += mm_nt(both[width:], hot)
+        acc[:, slots:] += mm_nt(both, hot_recv[step])
         return carry
 
-    lax.fori_loop(0, source.shape[0] // chunk, edges, 0)
+    lax.fori_loop(0, steps, edges, 0)
 
     slots_out[...] = mm_nt(eye(2 * cap), acc[width:, grid:slots].astype(BF)).astype(BF)
     backs = [
@@ -288,6 +294,8 @@
             pltpu.VMEM((2 * cap, width), BF),
             pltpu.VMEM((2 * width, slots + mesh_count), BF),
             pltpu.VMEM((2 * width, slots + mesh_count), F32),
+            pltpu.VMEM((edge_source.shape[0] // chunk, mesh_count, chunk), BF),
+            pltpu.VMEM((edge_source.shape[0] // chunk, 2 * width, chunk), F32),
             pltpu.VMEM((2 * cap, width), BF),
             pltpu.VMEM((2 * cap, width), BF),
             pltpu.VMEM((chans - 1, width, grid), BF),

time: 32.2 us -> 31.2 us (0.969)
  Pallas kernels: 31.4 us -> 30.4 us
    pallas_call x1, Pallas kernels: 30.6 us -> 29.6 us  [on_device(): pl.pallas_call(functools.partial(body, bands, chans, chunk), out_shape=(p...]
where the time goes in v4:
time: 31.2 us; the launch traced here: 31 us
  Pallas kernels  30.4 us (97%)
  between operations  0.64 us (2%)
    pallas_call x1, Pallas kernels, on_device(): pl.pallas_call(functools.partial(body, bands, chans, chunk), out_shape=(p...  29.6 us
    pallas_call x1, Pallas kernels, on_device(): pl.pallas_call(functools.partial(place, len(outs)), out_shape=tuple((jax....  0.83 us

profile of v4, /device:TPU:0, one launch (start us, length us, event | category | flops | bytes accessed | tf_op | source)
XLA Modules:
  0.0 31.0 jit_solution(7776617991377936539)
XLA Ops:
  0.6 29.6 %shard_map.120 = (bf16[96,256]{1,0:T(8,128)(2,1)S(1)}, f32[96,468]{1,0:T(8,128)S(1)}, f32[96,384]{1,0:T(8,128)S(1)}, f32[96,384]{1,0:T(8,128)S(1)}) custom-call(bf16[468,256]{1,0:T(8,128)(2,1)} %bitcast.8, bf16[468,384]{1,0:T(8,128)(2,1)} %embed_in.1, bf16[96,384]{1,0:T(8,128)(2,1)} %bitcast.9, bf16[96,384]{1,0:T(8,128)(2,1)} %bitcast.10, ...), custom_call_target="tpu_custom_call" | custom-call | tf_op jit(solution)/shard_map/pallas_call | solution.py:276
  30.2 0.8 %shard_map.121 = (bf16[96,256]{1,0:T(8,128)(2,1)}, f32[96,468]{1,0:T(8,128)}, f32[96,384]{1,0:T(8,128)}, f32[96,384]{1,0:T(8,128)}) custom-call(bf16[96,256]{1,0:T(8,128)(2,1)S(1)} %get-tuple-element.12.refs_0_, f32[96,468]{1,0:T(8,128)S(1)} %get-tuple-element.13.refs_1_, f32[96,384]{1,0:T(8,128)S(1)} %get-tuple-element.14.refs_2_, ...), custom_call_target="tpu_custom_call" | custom-call | tf_op jit(solution)/shard_map/pallas_call | solution.py:322
